TPU v7x, 512 devices: a whole 4x4x16 slice. The times are simulated.
512 devices in a mesh: slab: 32 (over z, core), sub: 16 (over x, y).
Axes of the slice: x: 4, y: 4, z: 16, core: 2. Of those that a mesh axis runs over, the one named last changes fastest.
Arguments:
- child_moments: bfloat16 [216, 524288], P(None, ('slab', 'sub')), may hold values from -6 to 6
- incoming: bfloat16 [216, 65536], P(None, ('slab', 'sub')), may hold values from -6 to 6
- m2m_ops: bfloat16 [8, 216, 216], replicated, may hold values from -0.15625 to 0.15625
- m2l_ops: bfloat16 [160, 216, 216], P('sub'), may hold values from -0.046875 to 0.046875
- l2l_ops: bfloat16 [8, 216, 216], replicated, may hold values from -0.4375 to 0.4375
- partners: int32 [160, 65536], P(None, ('slab', 'sub')), may hold values from -1 to 65535, as said below
Outputs:
- child_locals: float32 [216, 524288], P(None, ('slab', 'sub'))
Inputs may be any that keep to these rules, and one draw needn't show every extreme that they name: `partners`: cells are numbered in Morton order of bricks of the domain, each brick one cell wide along the first dimension; the source of a pair lies in the same slab as its target or in an adjacent one, that is its id divided by 128 * 16 differs from the target's by at most one. Pairs are those of the interaction list: source and target are not adjacent, their parents are.
All inputs are finite; a program needn't handle non-finite values.
Results may differ from a plain program's by a relative error of at most 0.0035.
Values may be sent and summed in bfloat16 or wider, within the bound.
A program may use at most 128 MiB of HBM per device.

v0:
```python
import jax
import jax.numpy as jnp
from jax import lax
from jax.sharding import PartitionSpec as P


def laid_out(parts, dim):
    lengths = list(parts.shape[1:])
    lengths[dim] *= parts.shape[0]
    return jnp.moveaxis(parts, 0, dim).reshape(lengths)


def sent_to_all(shard, axis):
    copies = jnp.broadcast_to(shard, (lax.axis_size(axis), *shard.shape))
    return lax.all_to_all(copies, axis, split_axis=0, concat_axis=0, tiled=True)


def gather_directly(shard, axis, dim):
    return laid_out(sent_to_all(shard, axis), dim)


def extended(block, sides, width):
    for axis, dim in sides:
        count = lax.axis_size(axis)
        forward = [(i, i + 1) for i in range(count - 1)]
        backward = [(target, source) for source, target in forward]
        low = lax.ppermute(
            lax.slice_in_dim(block, block.shape[dim] - width, None, axis=dim), axis, forward
        )
        high = lax.ppermute(lax.slice_in_dim(block, 0, width, axis=dim), axis, backward)
        block = jnp.concatenate([low, block, high], axis=dim)
    return block


def local(child_moments, incoming, m2m_ops, m2l_ops, l2l_ops, partners):
    order_cube = child_moments.shape[0]
    cell_count = child_moments.shape[1] // 8
    children = child_moments.reshape(order_cube, cell_count, 8)
    moments = jnp.einsum(
        "oij,jpo->ip", m2m_ops, children, preferred_element_type=jnp.float32
    ).astype(jnp.bfloat16)
    my_slab = lax.axis_index("slab")
    gathered = gather_directly(moments, "sub", 1)
    group_span = gathered.shape[1]
    window = extended(gathered, (("slab", 1),), group_span)
    window_start = (my_slab - 1) * group_span
    usable = partners >= 0
    offset_ids = jnp.where(usable, partners - window_start, 0)
    columns = jnp.take(window, offset_ids, axis=1)
    columns = jnp.where(usable[None, :, :], columns, jnp.zeros((), jnp.bfloat16))
    far_field = jnp.einsum(
        "bij,jbc->ic",
        lax.all_gather(m2l_ops, "sub", axis=0, tiled=True),
        columns,
        preferred_element_type=jnp.float32,
    )
    locals_all = (incoming.astype(jnp.float32) + far_field).astype(jnp.bfloat16)
    child_out = jnp.einsum("oij,jp->ipo", l2l_ops, locals_all, preferred_element_type=jnp.float32)
    return child_out.reshape(order_cube, cell_count * 8)


def solution(mesh):
    in_specs = (
        P(None, ("slab", "sub")),
        P(None, ("slab", "sub")),
        P(),
        P("sub", None, None),
        P(),
        P(None, ("slab", "sub")),
    )
    out_specs = P(None, ("slab", "sub"))
    return jax.shard_map(local, mesh=mesh, in_specs=in_specs, out_specs=out_specs, check_vma=False)
```

profile of v0, /device:TPU:1, one launch (start us, length us, event | category | flops | bytes accessed | tf_op | source)
XLA Modules:
  0.0 173.8 jit_solution(206420777266208340)
XLA Ops:
  6.5 0.0 copy-start
  6.5 0.0 copy-start.1
  6.5 0.0 all-gather.2.cloned.1.call-start
  6.5 0.7 all-gather.2.cloned.1.call-update
  7.3 1.2 copy.14
  8.5 1.6 fusion.17
  10.1 1.0 broadcast_in_dim.32
  11.1 7.6 %all-to-all-start = ((bf16[16,216,128]{2,1,0:T(8,128)(2,1)}), bf16[16,216,128]{2,1,0:T(8,128)(2,1)S(1)}, u32[]{:S(2)}, u32[]{:S(2)}) async-start(bf16[16,216,128]{2,1,0:T(8,128)(2,1)} %broadcast_in_dim.32), calls=%async_computation | async-start | bytes 1769472 | tf_op jit(solution)/shard_map/all_to_all | solution.py:15
  18.7 10.9 %all-to-all-done = bf16[16,216,128]{2,1,0:T(8,128)(2,1)S(1)} async-done(((bf16[16,216,128]{2,1,0:T(8,128)(2,1)}), bf16[16,216,128]{2,1,0:T(8,128)(2,1)S(1)}, u32[]{:S(2)}, u32[]{:S(2)}) %all-to-all-start) | async-done | bytes 884768 | tf_op jit(solution)/shard_map/all_to_all | solution.py:15
  29.5 0.5 copy.16
  30.1 1.3 copy.17
  31.3 9.2 %collective-permute-start = (bf16[216,2048]{1,0:T(8,128)(2,1)}, bf16[216,2048]{1,0:T(8,128)(2,1)}, u32[]{:S(2)}, u32[]{:S(2)}) collective-permute-start(bf16[216,2048]{1,0:T(8,128)(2,1)} %copy.17), channel_id=1, source_target_pairs={{0,16},{16,32},{32,48},{48,64},{64,80},{80,96},{96,112},{112,128},... | collective-permute-start | bytes 2654216 | tf_op jit(solution)/shard_map/ppermute | solution.py:27
  40.5 1.9 %collective-permute-start.1 = (bf16[216,2048]{1,0:T(8,128)(2,1)}, bf16[216,2048]{1,0:T(8,128)(2,1)}, u32[]{:S(2)}, u32[]{:S(2)}) collective-permute-start(bf16[216,2048]{1,0:T(8,128)(2,1)} %copy.17), channel_id=1, source_target_pairs={{16,0},{32,16},{48,32},{64,48},{80,64},{96,80},{112,96},{128,112},... | collective-permute-start | bytes 2654216 | tf_op jit(solution)/shard_map/ppermute | solution.py:30
  42.4 0.0 copy-done.1
  42.5 8.2 %collective-permute-done = bf16[216,2048]{1,0:T(8,128)(2,1)} collective-permute-done((bf16[216,2048]{1,0:T(8,128)(2,1)}, bf16[216,2048]{1,0:T(8,128)(2,1)}, u32[]{:S(2)}, u32[]{:S(2)}) %collective-permute-start) | collective-permute-done | bytes 884768 | tf_op jit(solution)/shard_map/ppermute | solution.py:27
  50.8 1.5 copy.19
  52.3 3.2 %collective-permute-done.1 = bf16[216,2048]{1,0:T(8,128)(2,1)} collective-permute-done((bf16[216,2048]{1,0:T(8,128)(2,1)}, bf16[216,2048]{1,0:T(8,128)(2,1)}, u32[]{:S(2)}, u32[]{:S(2)}) %collective-permute-start.1) | collective-permute-done | bytes 884768 | tf_op jit(solution)/shard_map/ppermute | solution.py:30
  55.5 2.2 %copy.20 = bf16[216,2048]{0,1:T(8,128)(2,1)} copy(bf16[216,2048]{1,0:T(8,128)(2,1)} %collective-permute-done.1) | data formatting | bytes 1769472 | tf_op jit(solution)/shard_map/ppermute | solution.py:30
  57.7 3.1 %pad_maximum_fusion = bf16[216,6144]{0,1:T(8,128)(2,1)} fusion(bf16[216,2048]{0,1:T(8,128)(2,1)} %copy.20, bf16[216,2048]{0,1:T(8,128)(2,1)S(1)} %bitcast.42, bf16[216,2048]{0,1:T(8,128)(2,1)S(1)} %copy.19), kind=kLoop, calls=%fused_computation.9 | loop fusion | flops 7962624 | bytes 5308416 | tf_op jit(solution)/shard_map/concatenate | solution.py:31
  60.9 78.5 %gather_fusion = bf16[20480,216]{1,0:T(8,128)(2,1)} fusion(bf16[216,6144]{0,1:T(8,128)(2,1)} %pad_maximum_fusion, s32[20480]{0:T(1024)S(1)} %bitcast_clamp_fusion), kind=kCustom, calls=%fused_computation | custom fusion | bytes 17776640 | tf_op jit(solution)/shard_map/jit(_take)/gather | solution.py:49
  139.4 0.0 copy-start.2
  139.4 13.2 %copy.21 = bf16[160,128,216]{1,2,0:T(8,128)(2,1)} copy(bf16[160,128,216]{2,1,0:T(8,128)(2,1)} %bitcast.40) | data formatting | bytes 17694720 | tf_op jit(solution)/shard_map/jit(_take)/gather | solution.py:49
  152.6 0.0 all-gather.2.cloned.1.call-done
  152.6 0.0 copy-done.2
  152.6 12.2 %fusion.18 = bf16[216,128,1]{1,0,2:T(8,128)(2,1)S(1)} fusion(bf16[160,216,216]{2,1,0:T(8,128)(2,1)} %all-gather.2.cloned.1.call-done, bf16[160,128,216]{1,2,0:T(8,128)(2,1)} %copy.21, pred[160,128]{1,0:T(8,128)(4,1)S(1)} %get-tuple-element.6, pred[160,128]{1,0:T(8,128)(4,1)S(1)} %get-tuple-element.5, bf16[216,128]{1,0:T(8,128)(2,1)S(1)} %copy-done.2), kind=kOutput, calls=%fused_computation.16 | convolution fusion | flops 1919960064 | bytes 23928832 | tf_op jit(solution)/shard_map/bij,jbc->ic/dot_general | solution.py:51
  164.8 0.0 copy-done
  164.8 0.4 convolution_bitcast_fusion
  165.2 0.5 copy.22
  165.7 1.2 copy.23
  (2 shorter events, 0.1 us)
Async XLA Ops:
  6.5 158.3 %copy-start = (bf16[8,216,216]{2,1,0:T(8,128)(2,1)S(1)}, bf16[8,216,216]{2,1,0:T(8,128)(2,1)}, u32[]{:S(2)}) copy-start(bf16[8,216,216]{2,1,0:T(8,128)(2,1)} %param.10) | copy-start | bytes 2239492
  6.5 35.9 %copy-start.1 = (s32[160,128]{1,0:T(8,128)S(1)}, s32[160,128]{1,0:T(8,128)}, u32[]{:S(2)}) copy-start(s32[160,128]{1,0:T(8,128)} %param.11) | copy-start | bytes 245764
  6.5 146.0 %all-gather.2.cloned.1.call-start = ((), (), s32[]{:S(2)}) async-start(), calls=%async_computation.1 | async-start | bytes 18800640 | tf_op jit(solution)/shard_map/all_gather | solution.py:53
  11.1 18.4 %all-to-all-start = ((bf16[16,216,128]{2,1,0:T(8,128)(2,1)}), bf16[16,216,128]{2,1,0:T(8,128)(2,1)S(1)}, u32[]{:S(2)}, u32[]{:S(2)}) async-start(bf16[16,216,128]{2,1,0:T(8,128)(2,1)} %broadcast_in_dim.32), calls=%async_computation | async-start | bytes 1769472 | tf_op jit(solution)/shard_map/all_to_all | solution.py:15
  31.3 19.5 %collective-permute-start = (bf16[216,2048]{1,0:T(8,128)(2,1)}, bf16[216,2048]{1,0:T(8,128)(2,1)}, u32[]{:S(2)}, u32[]{:S(2)}) collective-permute-start(bf16[216,2048]{1,0:T(8,128)(2,1)} %copy.17), channel_id=1, source_target_pairs={{0,16},{16,32},{32,48},{48,64},{64,80},{80,96},{96,112},{112,128},... | collective-permute-start | bytes 2654216 | tf_op jit(solution)/shard_map/ppermute | solution.py:27
  40.5 15.0 %collective-permute-start.1 = (bf16[216,2048]{1,0:T(8,128)(2,1)}, bf16[216,2048]{1,0:T(8,128)(2,1)}, u32[]{:S(2)}, u32[]{:S(2)}) collective-permute-start(bf16[216,2048]{1,0:T(8,128)(2,1)} %copy.17), channel_id=1, source_target_pairs={{16,0},{32,16},{48,32},{64,48},{80,64},{96,80},{112,96},{128,112},... | collective-permute-start | bytes 2654216 | tf_op jit(solution)/shard_map/ppermute | solution.py:30
  139.4 13.2 %copy-start.2 = (bf16[216,128]{1,0:T(8,128)(2,1)S(1)}, bf16[216,128]{1,0:T(8,128)(2,1)}, u32[]{:S(2)}) copy-start(bf16[216,128]{1,0:T(8,128)(2,1)} %param.7) | copy-start | bytes 165892
Sparse Core Ops, SparseCore 0:
  10.4 136.3 all-gather.1
where the time goes:
time: 176 us; the launch traced here: 174 us
  local copies, waits for them, and re-layouts  101 us (57%)
  waiting for transfers between devices  23 us (13%)
  starting transfers between devices  18.7 us (11%)
  matrix products  14.2 us (8%)
  between operations  13.5 us (8%)
  other arithmetic  3.21 us (2%)
    gather x2, local copies, waits for them, and re-layouts, local(): columns = jnp.take(window, offset_ids, axis=1)  91.7 us
    dot_general x1, matrix products, local(): jnp.einsum('bij,jbc->ic', lax.all_gather(m2l_ops, 'sub', axis=0, tiled=Tr...  12.2 us
    all_to_all x1, waiting for transfers between devices, sent_to_all(): return lax.all_to_all(copies, axis, split_axis=0, concat_axis=0, tiled=True)  10.9 us
    ppermute x1, starting transfers between devices, extended(): lax.ppermute(lax.slice_in_dim(block, block.shape[dim] - width, None, axis...  9.18 us
    ppermute x1, waiting for transfers between devices, extended(): lax.ppermute(lax.slice_in_dim(block, block.shape[dim] - width, None, axis...  8.24 us
    all_to_all x1, starting transfers between devices, sent_to_all(): return lax.all_to_all(copies, axis, split_axis=0, concat_axis=0, tiled=True)  7.57 us
  transfers between devices with their start and end apart: 4, of which 3 were waited for; matrix products, arithmetic and copies ran while one was open for 60% of the time, Pallas kernels for 0%

commit v1 on v0

v1 whole, which is shorter than its diff:
```python
import functools

import jax
import jax.numpy as jnp
from jax import lax
from jax.experimental import pallas as pl
from jax.experimental.pallas import tpu as pltpu
from jax.sharding import PartitionSpec as P

MESH = pl.DeviceIdType.MESH
F32 = jnp.float32
BF16 = jnp.bfloat16
VM = pl.BlockSpec(memory_space=pltpu.VMEM)
NONE = 64


def peers_of(sub, n_sub):
    side = 4
    steps = [(dx, dy) for dx in range(side) for dy in range(n_sub // side) if (dx, dy) != (0, 0)]
    steps.sort(key=lambda s: min(s[0], 4 - s[0]) + min(s[1], 4 - s[1]))
    return steps


def moved(sub, step, sign):
    x, y = sub // 4, sub % 4
    return (x + sign * step[0] + 4) % 4 * 4 + (y + sign * step[1] + 4) % 4


def exchange_kernel(n_slab, n_sub, per, child_ref, m2m_ref, partners_ref, win_ref, words_ref, table_ref,
                    block, mine, w_send, w_recv, b_send, b_recv, lo_send, lo_recv, hi_send, hi_recv, own_sem):
    slab = lax.axis_index("slab")
    sub = lax.axis_index("sub")
    lower = (slab + n_slab - 1) % n_slab
    upper = (slab + 1) % n_slab
    steps = peers_of(sub, n_sub)
    cells = block.shape[1]

    barrier = pltpu.get_barrier_semaphore()
    for step in steps:
        pl.semaphore_signal(barrier, inc=1, device_id={"slab": slab, "sub": moved(sub, step, 1)}, device_id_type=MESH)
    for other in (lower, upper):
        pl.semaphore_signal(barrier, inc=1, device_id={"slab": other, "sub": sub}, device_id_type=MESH)

    base = (slab - 1) * (n_sub * cells)
    lane = lax.broadcasted_iota(jnp.int32, (per, cells), 1)
    for j in range(n_sub):
        p = partners_ref[per * j : per * (j + 1), :]
        rel = p - base
        brick = jnp.where(p >= 0, jnp.right_shift(rel, 7), NONE)
        code = jnp.full(p.shape, 512, jnp.int32)
        packed = jnp.zeros(p.shape, jnp.int32)
        last = jnp.full((per, 1), -1, jnp.int32)
        for c in range(4):
            last = jnp.min(jnp.where(brick > last, brick, NONE), axis=1, keepdims=True)
            code = jnp.where((brick == last) & (brick < NONE), c * 128 + jnp.bitwise_and(rel, 127), code)
            packed = jnp.where(lane % 4 == c, jnp.where(last < NONE, last, n_sub), packed)
        mine[j, 0:per, :] = code + packed * 1024
        mine[j, per:16, :] = jnp.full((16 - per, cells), 512, jnp.int32)

    diff = lax.broadcasted_iota(jnp.int32, (8 * cells, cells), 0) - 8 * lax.broadcasted_iota(jnp.int32, (8 * cells, cells), 1)
    children = child_ref[...]
    total = jnp.zeros((block.shape[0], cells), F32)
    for o in range(8):
        pick = jnp.where(diff == o, 1.0, 0.0).astype(BF16)
        column = jnp.dot(children, pick, preferred_element_type=F32).astype(BF16)
        total += jnp.dot(m2m_ref[o], column, preferred_element_type=F32)
    block[...] = total.astype(BF16)

    pl.semaphore_wait(barrier, len(steps) + 2)

    copies = []

    def send(src, dst, send_sem, recv_sem, device):
        copy = pltpu.make_async_remote_copy(
            src_ref=src, dst_ref=dst, send_sem=send_sem, recv_sem=recv_sem, device_id=device, device_id_type=MESH
        )
        copy.start()
        copies.append(copy)

    own = pltpu.make_async_copy(block, win_ref.at[n_sub + sub], own_sem.at[0])
    own.start()
    own_words = pltpu.make_async_copy(mine.at[sub], words_ref.at[sub], own_sem.at[1])
    own_words.start()
    for d, step in enumerate(steps):
        to = moved(sub, step, 1)
        send(block, win_ref.at[n_sub + sub], b_send.at[d], b_recv.at[d], {"slab": slab, "sub": to})
        if d == 0:
            send(block, win_ref.at[2 * n_sub + sub], lo_send.at[15], lo_recv.at[15], {"slab": lower, "sub": sub})
            send(block, win_ref.at[sub], hi_send.at[15], hi_recv.at[15], {"slab": upper, "sub": sub})
    for d, step in enumerate(steps):
        to = moved(sub, step, 1)
        send(mine.at[to], words_ref.at[sub], w_send.at[d], w_recv.at[d], {"slab": slab, "sub": to})
    for d, step in enumerate(steps):
        origin = moved(sub, step, -1)
        arrived = pltpu.make_async_remote_copy(
            src_ref=block, dst_ref=win_ref.at[n_sub + origin], send_sem=b_send.at[d], recv_sem=b_recv.at[d],
            device_id={"slab": slab, "sub": origin}, device_id_type=MESH,
        )
        arrived.wait_recv()
        place = win_ref.at[n_sub + origin]
        send(place, win_ref.at[2 * n_sub + origin], lo_send.at[d], lo_recv.at[d], {"slab": lower, "sub": sub})
        send(place, win_ref.at[origin], hi_send.at[d], hi_recv.at[d], {"slab": upper, "sub": sub})
    own.wait()
    own_words.wait()
    for d, step in enumerate(steps):
        origin = moved(sub, step, -1)
        pltpu.make_async_remote_copy(
            src_ref=mine.at[0], dst_ref=words_ref.at[origin], send_sem=w_send.at[d], recv_sem=w_recv.at[d],
            device_id={"slab": slab, "sub": origin}, device_id_type=MESH,
        ).wait_recv()
    flat = jnp.concatenate([words_ref[j] for j in range(n_sub)], axis=0)
    table_ref[...] = jnp.right_shift(jnp.transpose(flat)[0:8, :], 10)
    for d in range(16):
        origin = sub if d == 15 else moved(sub, steps[d], -1)
        pltpu.make_async_remote_copy(
            src_ref=block, dst_ref=win_ref.at[2 * n_sub + origin], send_sem=lo_send.at[d], recv_sem=lo_recv.at[d],
            device_id={"slab": upper, "sub": sub}, device_id_type=MESH,
        ).wait_recv()
        pltpu.make_async_remote_copy(
            src_ref=block, dst_ref=win_ref.at[origin], send_sem=hi_send.at[d], recv_sem=hi_recv.at[d],
            device_id={"slab": lower, "sub": sub}, device_id_type=MESH,
        ).wait_recv()
    for copy in copies:
        copy.wait_send()


def transfer_kernel(per, table_ref, win_ref, words_ref, ops_ref, part_ref):
    rows, cells = part_ref.shape[1:]

    def brick(b, carry):
        total = jnp.zeros((rows, cells), F32)
        for k in range(per):
            code = jnp.bitwise_and(words_ref[b][k : k + 1, :], 1023)
            place = jnp.broadcast_to(jnp.bitwise_and(code, 127), (rows, cells))
            which = jnp.right_shift(code, 7)
            columns = jnp.zeros((rows, cells), F32)
            for c in range(4):
                source = win_ref[table_ref[c, b * 16 + k]].astype(F32)
                got = jnp.take_along_axis(source, place, axis=1, mode="promise_in_bounds")
                columns = jnp.where(which == c, got, columns)
            total += jnp.dot(ops_ref[k], columns.astype(BF16), preferred_element_type=F32)
        part_ref[b] = total.astype(BF16)
        return carry

    lax.fori_loop(0, part_ref.shape[0], brick, 0)


def finish_kernel(n_sub, part_ref, incoming_ref, l2l_ref, out_ref, got, p_send, p_recv):
    slab = lax.axis_index("slab")
    sub = lax.axis_index("sub")
    steps = peers_of(sub, n_sub)
    cells = incoming_ref.shape[1]
    barrier = pltpu.get_barrier_semaphore()
    for step in steps:
        pl.semaphore_signal(barrier, inc=1, device_id={"slab": slab, "sub": moved(sub, step, 1)}, device_id_type=MESH)
    pl.semaphore_wait(barrier, len(steps))
    copies = []
    for d, step in enumerate(steps):
        to = moved(sub, step, 1)
        copy = pltpu.make_async_remote_copy(
            src_ref=part_ref.at[to], dst_ref=got.at[d], send_sem=p_send.at[d], recv_sem=p_recv.at[d],
            device_id={"slab": slab, "sub": to}, device_id_type=MESH,
        )
        copy.start()
        copies.append(copy)
    total = part_ref[sub].astype(F32)
    for d, copy in enumerate(copies):
        copy.wait_recv()
        total += got[d].astype(F32)
    local = (incoming_ref[...].astype(F32) + total).astype(BF16)
    wide = 256
    for g in range(8 * cells // wide):
        row = lax.broadcasted_iota(jnp.int32, (cells, wide), 0)
        column = lax.broadcasted_iota(jnp.int32, (cells, wide), 1) + g * wide
        spread = jnp.where(jnp.right_shift(column, 3) == row, 1.0, 0.0).astype(BF16)
        repeated = jnp.dot(local, spread, preferred_element_type=F32)
        octant = jnp.bitwise_and(lax.broadcasted_iota(jnp.int32, repeated.shape, 1), 7)
        result = jnp.zeros(repeated.shape, F32)
        for o in range(8):
            kept = jnp.where(octant == o, repeated, 0.0).astype(BF16)
            result += jnp.dot(l2l_ref[o], kept, preferred_element_type=F32)
        out_ref[:, g * wide : (g + 1) * wide] = result
    for copy in copies:
        copy.wait_send()


def solution(mesh):
    n_slab, n_sub = mesh.shape["slab"], mesh.shape["sub"]
    dma = pltpu.SemaphoreType.DMA

    def local(child_moments, incoming, m2m_ops, m2l_ops, l2l_ops, partners):
        rows = child_moments.shape[0]
        cells = incoming.shape[1]
        per = m2l_ops.shape[0]
        win, words, table = pl.pallas_call(
            functools.partial(exchange_kernel, n_slab, n_sub, per),
            name="exchange",
            out_shape=(
                jax.ShapeDtypeStruct((3 * n_sub, rows, cells), BF16),
                jax.ShapeDtypeStruct((n_sub, 16, cells), jnp.int32),
                jax.ShapeDtypeStruct((8, n_sub * 16), jnp.int32),
            ),
            in_specs=[VM] * 3,
            out_specs=(VM, VM, VM),
            scratch_shapes=[
                pltpu.VMEM((rows, cells), BF16),
                pltpu.VMEM((n_sub, 16, cells), jnp.int32),
            ]
            + [dma((16,))] * 8
            + [dma((2,))],
            compiler_params=pltpu.CompilerParams(collective_id=0, has_side_effects=True, vmem_limit_bytes=24 * 2**20),
        )(child_moments, m2m_ops, partners)
        part = pl.pallas_call(
            functools.partial(transfer_kernel, per),
            name="transfer",
            out_shape=jax.ShapeDtypeStruct((n_sub, rows, cells), BF16),
            in_specs=[pl.BlockSpec(memory_space=pltpu.SMEM)] + [VM] * 3,
            out_specs=VM,
            compiler_params=pltpu.CompilerParams(vmem_limit_bytes=24 * 2**20),
        )(table, win, words, m2l_ops)
        return pl.pallas_call(
            functools.partial(finish_kernel, n_sub),
            name="finish",
            out_shape=jax.ShapeDtypeStruct((rows, 8 * cells), F32),
            in_specs=[VM] * 3,
            out_specs=VM,
            scratch_shapes=[pltpu.VMEM((n_sub - 1, rows, cells), BF16), dma((16,)), dma((16,))],
            compiler_params=pltpu.CompilerParams(collective_id=1, has_side_effects=True, vmem_limit_bytes=24 * 2**20),
        )(part, incoming, l2l_ops)

    in_specs = (
        P(None, ("slab", "sub")),
        P(None, ("slab", "sub")),
        P(),
        P("sub", None, None),
        P(),
        P(None, ("slab", "sub")),
    )
    return jax.shard_map(local, mesh=mesh, in_specs=in_specs, out_specs=P(None, ("slab", "sub")), check_vma=False)
```

time: 176 us -> 67 us (0.38)
  the two profiles are of different devices: /device:TPU:1 before, /device:TPU:16 now
where the time goes in v1:
time: 67 us; the launch traced here: 66.8 us
  Pallas kernels  61.5 us (92%)
  local copies, waits for them, and re-layouts  5.23 us (8%)
    pallas_call x1, Pallas kernels, local(): pl.pallas_call(functools.partial(exchange_kernel, n_slab, n_sub, per), na...  28.9 us
    pallas_call x1, Pallas kernels, local(): pl.pallas_call(functools.partial(finish_kernel, n_sub), name='finish', ou...  17.5 us
    pallas_call x1, Pallas kernels, local(): pl.pallas_call(functools.partial(transfer_kernel, per), name='transfer',...  15.1 us
    unnamed x13, local copies, waits for them, and re-layouts  5.23 us

profile of v1, /device:TPU:16, one launch (start us, length us, event | category | flops | bytes accessed | tf_op | source)
XLA Modules:
  0.0 66.8 jit_solution(10511594398561877023)
XLA Ops:
  0.0 0.0 copy-start.2
  0.0 1.2 %copy-done.2 = bf16[8,216,216]{2,1,0:T(8,128)(2,1)S(1)} copy-done((bf16[8,216,216]{2,1,0:T(8,128)(2,1)S(1)}, bf16[8,216,216]{2,1,0:T(8,128)(2,1)}, u32[]{:S(2)}) %copy-start.2) | copy-done | bytes 746520
  1.2 0.0 copy-start.3
  1.2 1.0 %copy-done.3 = bf16[216,1024]{1,0:T(8,128)(2,1)S(1)} copy-done((bf16[216,1024]{1,0:T(8,128)(2,1)S(1)}, bf16[216,1024]{1,0:T(8,128)(2,1)}, u32[]{:S(2)}) %copy-start.3) | copy-done | bytes 442392
  2.2 0.0 copy-start.4
  2.2 0.9 %copy-done.4 = s32[160,128]{1,0:T(8,128)S(1)} copy-done((s32[160,128]{1,0:T(8,128)S(1)}, s32[160,128]{1,0:T(8,128)}, u32[]{:S(2)}) %copy-start.4) | copy-done | bytes 81944
  3.1 0.0 copy-start.1
  3.1 0.0 copy-start.5
  3.1 28.9 %exchange.1 = (bf16[48,216,128]{2,1,0:T(8,128)(2,1)S(1)}, s32[16,16,128]{2,1,0:T(8,128)S(1)}, s32[8,256]{1,0:T(8,128)S(1)}) custom-call(bf16[216,1024]{1,0:T(8,128)(2,1)S(1)} %copy-done.3, bf16[8,216,216]{2,1,0:T(8,128)(2,1)S(1)} %copy-done.2, s32[160,128]{1,0:T(8,128)S(1)} %copy-done.4), custom_call_target="tpu_custom_call" | custom-call | tf_op jit(solution)/shard_map/exchange/pallas_call | solution.py:195
  32.0 0.0 copy-start
  32.0 1.2 %copy-done = bf16[10,216,216]{2,1,0:T(8,128)(2,1)S(1)} copy-done((bf16[10,216,216]{2,1,0:T(8,128)(2,1)S(1)}, bf16[10,216,216]{2,1,0:T(8,128)(2,1)}, u32[]{:S(2)}) %copy-start) | copy-done | bytes 933144
  33.2 15.1 %transfer.1.part_ref = bf16[16,216,128]{2,1,0:T(8,128)(2,1)S(1)} custom-call(s32[8,256]{1,0:T(8,128)S(1)} %get-tuple-element.8.table_ref, bf16[48,216,128]{2,1,0:T(8,128)(2,1)S(1)} %get-tuple-element.9.win_ref, s32[16,16,128]{2,1,0:T(8,128)S(1)} %get-tuple-element.10.words_ref, bf16[10,216,216]{2,1,0:T(8,128)(2,1)S(1)} %copy-done), custom_call_target="tpu_custom_call" | custom-call | tf_op jit(solution)/shard_map/transfer/pallas_call | solution.py:213
  48.3 0.0 copy-done.1
  48.3 0.0 copy-done.5
  48.3 17.5 %finish.1 = f32[216,1024]{1,0:T(8,128)S(1)} custom-call(bf16[16,216,128]{2,1,0:T(8,128)(2,1)S(1)} %transfer.1.part_ref, bf16[216,128]{1,0:T(8,128)(2,1)S(1)} %copy-done.5, bf16[8,216,216]{2,1,0:T(8,128)(2,1)S(1)} %copy-done.1), custom_call_target="tpu_custom_call" | custom-call | tf_op jit(solution)/shard_map/finish/pallas_call | solution.py:221
  65.8 0.9 %copy.8 = f32[216,1024]{1,0:T(8,128)} copy(f32[216,1024]{1,0:T(8,128)S(1)} %finish.1) | data formatting | bytes 1769472
Async XLA Ops:
  0.0 1.2 %copy-start.2 = (bf16[8,216,216]{2,1,0:T(8,128)(2,1)S(1)}, bf16[8,216,216]{2,1,0:T(8,128)(2,1)}, u32[]{:S(2)}) copy-start(bf16[8,216,216]{2,1,0:T(8,128)(2,1)} %m2m_ref.1) | copy-start | bytes 2239492
  1.2 1.0 %copy-start.3 = (bf16[216,1024]{1,0:T(8,128)(2,1)S(1)}, bf16[216,1024]{1,0:T(8,128)(2,1)}, u32[]{:S(2)}) copy-start(bf16[216,1024]{1,0:T(8,128)(2,1)} %child_ref.1) | copy-start | bytes 1327108
  2.2 0.9 %copy-start.4 = (s32[160,128]{1,0:T(8,128)S(1)}, s32[160,128]{1,0:T(8,128)}, u32[]{:S(2)}) copy-start(s32[160,128]{1,0:T(8,128)} %partners_ref.1) | copy-start | bytes 245764
  3.1 45.2 %copy-start.1 = (bf16[8,216,216]{2,1,0:T(8,128)(2,1)S(1)}, bf16[8,216,216]{2,1,0:T(8,128)(2,1)}, u32[]{:S(2)}) copy-start(bf16[8,216,216]{2,1,0:T(8,128)(2,1)} %l2l_ref.1) | copy-start | bytes 2239492
  3.1 45.2 %copy-start.5 = (bf16[216,128]{1,0:T(8,128)(2,1)S(1)}, bf16[216,128]{1,0:T(8,128)(2,1)}, u32[]{:S(2)}) copy-start(bf16[216,128]{1,0:T(8,128)(2,1)} %incoming_ref.1) | copy-start | bytes 165892
  32.0 1.2 %copy-start = (bf16[10,216,216]{2,1,0:T(8,128)(2,1)S(1)}, bf16[10,216,216]{2,1,0:T(8,128)(2,1)}, u32[]{:S(2)}) copy-start(bf16[10,216,216]{2,1,0:T(8,128)(2,1)} %ops_ref.1) | copy-start | bytes 2799364

commit v2 on v0

v2 whole, which is shorter than its diff:
```python
import functools

import jax
import jax.numpy as jnp
from jax import lax
from jax.experimental import pallas as pl
from jax.experimental.pallas import tpu as pltpu
from jax.sharding import PartitionSpec as P

MESH = pl.DeviceIdType.MESH
F32 = jnp.float32
BF16 = jnp.bfloat16
VM = pl.BlockSpec(memory_space=pltpu.VMEM)
HB = pl.BlockSpec(memory_space=pltpu.HBM)
NONE = 64


def hops(i):
    return min(i // 4, 4 - i // 4) + min(i % 4, 4 - i % 4)


ORDER = sorted(range(1, 16), key=hops)


def moved(sub, i, sign):
    x, y = sub // 4, sub % 4
    return (x + sign * (i // 4) + 4) % 4 * 4 + (y + sign * (i % 4) + 4) % 4


def main_kernel(n_slab, n_sub, per, child_hbm, incoming_hbm, m2m_hbm, ops_hbm, partners_hbm, local_ref,
                child_ref, incoming_ref, m2m_ref, ops_ref, partners_ref, in_sem,
                block, win_ref, mine, words_ref, table_ref, table_smem, part_ref, got,
                w_send, w_recv, b_send, b_recv, lo_send, lo_recv, hi_send, hi_recv, p_send, p_recv, own_sem):
    slab = lax.axis_index("slab")
    sub = lax.axis_index("sub")
    lower = (slab + n_slab - 1) % n_slab
    upper = (slab + 1) % n_slab
    rows, cells = block.shape

    loads = [
        pltpu.make_async_copy(source, target, in_sem.at[i])
        for i, (source, target) in enumerate(
            [(partners_hbm, partners_ref), (child_hbm, child_ref), (m2m_hbm, m2m_ref), (ops_hbm, ops_ref), (incoming_hbm, incoming_ref)]
        )
    ]
    for load in loads:
        load.start()
    barrier = pltpu.get_barrier_semaphore()
    for i in range(1, n_sub):
        pl.semaphore_signal(barrier, inc=1, device_id={"slab": slab, "sub": moved(sub, i, 1)}, device_id_type=MESH)
    for other in (lower, upper):
        pl.semaphore_signal(barrier, inc=1, device_id={"slab": other, "sub": sub}, device_id_type=MESH)

    diff = lax.broadcasted_iota(jnp.int32, (8 * cells, cells), 0) - 8 * lax.broadcasted_iota(jnp.int32, (8 * cells, cells), 1)
    loads[1].wait()
    children = child_ref[...]
    columns = []
    for o in range(0, 8, 2):
        pick = jnp.concatenate([jnp.where(diff == q, 1.0, 0.0).astype(BF16) for q in (o, o + 1)], axis=1)
        both = jnp.dot(children, pick, preferred_element_type=F32).astype(BF16)
        columns += [both[:, :cells], both[:, cells:]]
    loads[2].wait()
    total = jnp.zeros((rows, cells), F32)
    for o in range(8):
        total += jnp.dot(m2m_ref[o], columns[o], preferred_element_type=F32)
    moments = total.astype(BF16)
    block[...] = moments
    win_ref[n_sub + sub] = moments
    pl.semaphore_wait(barrier, n_sub + 1)

    copies = []

    def send(src, dst, send_sem, recv_sem, device):
        copy = pltpu.make_async_remote_copy(
            src_ref=src, dst_ref=dst, send_sem=send_sem, recv_sem=recv_sem, device_id=device, device_id_type=MESH
        )
        copy.start()
        copies.append(copy)

    def expect(dst, send_sem, recv_sem, device):
        pltpu.make_async_remote_copy(
            src_ref=dst, dst_ref=dst, send_sem=send_sem, recv_sem=recv_sem, device_id=device, device_id_type=MESH
        ).wait_recv()

    for i in ORDER:
        if i == ORDER[4]:
            send(block, win_ref.at[2 * n_sub + sub], lo_send.at[0], lo_recv.at[0], {"slab": lower, "sub": sub})
            send(block, win_ref.at[sub], hi_send.at[0], hi_recv.at[0], {"slab": upper, "sub": sub})
        send(block, win_ref.at[n_sub + sub], b_send.at[i], b_recv.at[i], {"slab": slab, "sub": moved(sub, i, 1)})

    loads[0].wait()
    base = (slab - 1) * (n_sub * cells)
    lane = lax.broadcasted_iota(jnp.int32, (per, cells), 1)
    place = lax.broadcasted_iota(jnp.int32, (cells, cells), 0)
    across = lax.broadcasted_iota(jnp.int32, (cells, cells), 1)

    def words_for(group):
        codes, tables, which_of = [], [], []
        for j in range(8 * group, 8 * group + 8):
            p = partners_ref[per * j : per * (j + 1), :]
            rel = p - base
            brick = jnp.where(p >= 0, jnp.right_shift(rel, 7), NONE)
            which = jnp.zeros(p.shape, jnp.int32)
            packed = jnp.zeros(p.shape, jnp.int32)
            last = jnp.full((per, 1), -1, jnp.int32)
            for c in range(4):
                last = jnp.min(jnp.where(brick > last, brick, NONE), axis=1, keepdims=True)
                which = jnp.where((brick == last) & (brick < NONE), c, which)
                packed = jnp.where(lane % 4 == c, jnp.where(last < NONE, last, n_sub), packed)
            codes.append(jnp.where(p >= 0, jnp.bitwise_and(rel, 127) + 128, 0))
            tables.append(packed)
            which_of.append(which.astype(F32))
            which_of.append(jnp.zeros((16 - per, cells), F32))
        turned = jnp.transpose(jnp.concatenate(which_of, axis=0))
        back = jnp.zeros((cells, cells), F32)
        for j in range(8):
            left, right = [], []
            for k in range(per):
                left.append(jnp.where(jnp.bitwise_and(codes[j][k : k + 1, :], 127) == place, 1.0, 0.0).astype(BF16))
                right.append(jnp.where(across == 16 * j + k, turned, 0.0).astype(BF16))
            back += jnp.dot(jnp.concatenate(left, axis=1), jnp.concatenate(right, axis=0), preferred_element_type=F32)
        back = jnp.transpose(back).astype(jnp.int32)
        for j in range(8):
            mine[8 * group + j, 0:per, :] = codes[j] + jnp.bitwise_and(back[16 * j : 16 * j + per, :], 3) * 256 + tables[j] * 1024
            mine[8 * group + j, per:16, :] = jnp.zeros((16 - per, cells), jnp.int32)

    words_for(0)
    for n, i in enumerate(ORDER):
        origin = moved(sub, i, -1)
        expect(win_ref.at[n_sub + origin], b_send.at[i], b_recv.at[i], {"slab": slab, "sub": origin})
        source = win_ref.at[n_sub + origin]
        send(source, win_ref.at[2 * n_sub + origin], lo_send.at[i], lo_recv.at[i], {"slab": lower, "sub": sub})
        send(source, win_ref.at[origin], hi_send.at[i], hi_recv.at[i], {"slab": upper, "sub": sub})
        if n == 5:
            words_for(1)
    for i in ORDER:
        to = moved(sub, i, 1)
        send(mine.at[to], words_ref.at[sub], w_send.at[i], w_recv.at[i], {"slab": slab, "sub": to})
    words_ref[sub] = mine[sub]
    for i in ORDER:
        origin = moved(sub, i, -1)
        expect(words_ref.at[origin], w_send.at[i], w_recv.at[i], {"slab": slab, "sub": origin})
    flat = jnp.concatenate([words_ref[j] for j in range(n_sub)], axis=0)
    table_ref[...] = jnp.minimum(jnp.bitwise_and(jnp.right_shift(jnp.transpose(flat)[0:8, :], 10), 63), 3 * n_sub - 1)
    to_smem = pltpu.make_async_copy(table_ref, table_smem, own_sem.at[0])
    to_smem.start()
    loads[3].wait()
    to_smem.wait()
    for i in [0] + ORDER:
        origin = moved(sub, i, -1)
        expect(win_ref.at[2 * n_sub + origin], lo_send.at[i], lo_recv.at[i], {"slab": upper, "sub": sub})
        expect(win_ref.at[origin], hi_send.at[i], hi_recv.at[i], {"slab": lower, "sub": sub})

    def columns_of(b, k):
        word = words_ref[b][k : k + 1, :]
        local = jnp.broadcast_to(jnp.bitwise_and(word, 127), (rows, cells))
        which = jnp.broadcast_to(jnp.bitwise_and(jnp.right_shift(word, 8), 3), (rows, cells)).astype(jnp.int16)
        there = jnp.broadcast_to(jnp.bitwise_and(word, 128), (rows, cells)).astype(jnp.int16)
        merged = win_ref[table_smem[0, b * 16 + k]]
        for c in range(1, 4):
            merged = jnp.where(which == c, win_ref[table_smem[c, b * 16 + k]], merged)
        got = jnp.take_along_axis(merged.astype(F32), local, axis=1, mode="promise_in_bounds").astype(BF16)
        return jnp.where(there != 0, got, jnp.zeros((), BF16))

    def part_copy(i, target):
        return pltpu.make_async_remote_copy(
            src_ref=part_ref.at[i], dst_ref=got.at[i], send_sem=p_send.at[i], recv_sem=p_recv.at[i],
            device_id={"slab": slab, "sub": target}, device_id_type=MESH,
        )

    def two_bricks(n, carry):
        ids = [15 - 2 * n, 14 - 2 * n]
        bricks = [moved(sub, i, 1) for i in ids]
        total = jnp.zeros((rows, 2 * cells), F32)
        for k in range(per):
            both = jnp.concatenate([columns_of(b, k) for b in bricks], axis=1)
            total += jnp.dot(ops_ref[k], both, preferred_element_type=F32)
        for q, (i, b) in enumerate(zip(ids, bricks)):
            part_ref[i] = total[:, q * cells : (q + 1) * cells].astype(BF16)

            @pl.when(i != 0)
            def _():
                part_copy(i, b).start()

        return carry

    lax.fori_loop(0, n_sub // 2, two_bricks, 0)
    loads[4].wait()
    total = part_ref[0].astype(F32)
    for i in reversed(ORDER):
        part_copy(i, moved(sub, i, -1)).wait_recv()
        total += got[i].astype(F32)
    local_ref[...] = (incoming_ref[...].astype(F32) + total).astype(BF16)
    for i in ORDER:
        part_copy(i, moved(sub, i, 1)).wait_send()
    for copy in copies:
        copy.wait_send()


def children_kernel(local_ref, l2l_ref, out_ref):
    rows, wide = out_ref.shape
    cells = local_ref.shape[1]
    row = lax.broadcasted_iota(jnp.int32, (cells, wide), 0)
    column = lax.broadcasted_iota(jnp.int32, (cells, wide), 1) + pl.program_id(0) * wide
    spread = jnp.where(jnp.right_shift(column, 3) == row, 1.0, 0.0).astype(BF16)
    repeated = jnp.dot(local_ref[...], spread, preferred_element_type=F32)
    octant = jnp.bitwise_and(lax.broadcasted_iota(jnp.int32, repeated.shape, 1), 7)
    result = jnp.zeros(repeated.shape, F32)
    for o in range(8):
        kept = jnp.where(octant == o, repeated, 0.0).astype(BF16)
        result += jnp.dot(l2l_ref[o], kept, preferred_element_type=F32)
    out_ref[...] = result


def solution(mesh):
    n_slab, n_sub = mesh.shape["slab"], mesh.shape["sub"]
    dma = pltpu.SemaphoreType.DMA

    def local(child_moments, incoming, m2m_ops, m2l_ops, l2l_ops, partners):
        rows = child_moments.shape[0]
        cells = incoming.shape[1]
        per = m2l_ops.shape[0]
        locals_all = pl.pallas_call(
            functools.partial(main_kernel, n_slab, n_sub, per),
            name="main",
            out_shape=jax.ShapeDtypeStruct((rows, cells), BF16),
            in_specs=[HB] * 5,
            out_specs=VM,
            scratch_shapes=[pltpu.VMEM(a.shape, a.dtype) for a in (child_moments, incoming, m2m_ops, m2l_ops, partners)]
            + [
                dma((5,)),
                pltpu.VMEM((rows, cells), BF16),
                pltpu.VMEM((3 * n_sub, rows, cells), BF16),
                pltpu.VMEM((n_sub, 16, cells), jnp.int32),
                pltpu.VMEM((n_sub, 16, cells), jnp.int32),
                pltpu.VMEM((8, n_sub * 16), jnp.int32),
                pltpu.SMEM((8, n_sub * 16), jnp.int32),
                pltpu.VMEM((n_sub, rows, cells), BF16),
                pltpu.VMEM((n_sub, rows, cells), BF16),
            ]
            + [dma((16,))] * 10
            + [dma((1,))],
            compiler_params=pltpu.CompilerParams(collective_id=0, has_side_effects=True, vmem_limit_bytes=66_200_000),
        )(child_moments, incoming, m2m_ops, m2l_ops, partners)
        wide = 256
        return pl.pallas_call(
            children_kernel,
            name="children",
            out_shape=jax.ShapeDtypeStruct((rows, 8 * cells), F32),
            grid=(8 * cells // wide,),
            in_specs=[VM, VM],
            out_specs=pl.BlockSpec((rows, wide), lambda g: (0, g)),
            compiler_params=pltpu.CompilerParams(vmem_limit_bytes=16 * 2**20),
        )(locals_all, l2l_ops)

    in_specs = (
        P(None, ("slab", "sub")),
        P(None, ("slab", "sub")),
        P(),
        P("sub", None, None),
        P(),
        P(None, ("slab", "sub")),
    )
    return jax.shard_map(local, mesh=mesh, in_specs=in_specs, out_specs=P(None, ("slab", "sub")), check_vma=False)
```

time: 176 us -> 48.7 us (0.28)
  local copies, waits for them, and re-layouts: 101 us -> 1.98 us
  Pallas kernels: 0 us -> 46 us
  waiting for transfers between devices: 23 us -> 0 us
  starting transfers between devices: 18.7 us -> 0 us
  matrix products: 14.2 us -> 0 us
  between operations: 13.5 us -> 0.02 us
  other arithmetic: 3.21 us -> 0 us
    gather x2 -> x0, local copies, waits for them, and re-layouts: 91.7 us -> none  [local(): columns = jnp.take(window, offset_ids, axis=1)]
    pallas_call x0 -> x2, Pallas kernels: none -> 46 us  [the longest x1 42.9 us: local(): pl.pallas_call(functools.partial(main_kernel, n_slab, n_sub, per), name='...]
    dot_general x3 -> x0, matrix products: 14.2 us -> none  [the longest x1 12.2 us: local(): jnp.einsum('bij,jbc->ic', lax.all_gather(m2l_ops, 'sub', axis=0, tiled=Tr...]
    ppermute x2 -> x0, waiting for transfers between devices: 11.5 us -> none  [the longest x1 8.24 us: extended(): lax.ppermute(lax.slice_in_dim(block, block.shape[dim] - width, None, axis...]
    ppermute x2 -> x0, starting transfers between devices: 11.1 us -> none  [the longest x1 9.18 us: extended(): lax.ppermute(lax.slice_in_dim(block, block.shape[dim] - width, None, axis...]
    all_to_all x1 -> x0, waiting for transfers between devices: 10.9 us -> none  [sent_to_all(): return lax.all_to_all(copies, axis, split_axis=0, concat_axis=0, tiled=True)]
    all_to_all x1 -> x0, starting transfers between devices: 7.57 us -> none  [sent_to_all(): return lax.all_to_all(copies, axis, split_axis=0, concat_axis=0, tiled=True)]
    ppermute x2 -> x0, local copies, waits for them, and re-layouts: 3.7 us -> none  [the longest x1 2.24 us: extended(): lax.ppermute(lax.slice_in_dim(block, 0, width, axis=dim), axis, backward)]
  transfers between devices with their start and end apart: 4 -> 0, of which waited for: 3 -> 0; matrix products, arithmetic and copies ran while one was open for 60% -> 0% of each run, Pallas kernels for 0% -> 0%
where the time goes in v2:
time: 48.7 us; the launch traced here: 48 us
  Pallas kernels  46 us (94%)
  local copies, waits for them, and re-layouts  1.98 us (4%)
    pallas_call x1, Pallas kernels, local(): pl.pallas_call(functools.partial(main_kernel, n_slab, n_sub, per), name='...  42.9 us
    pallas_call x1, Pallas kernels, local(): pl.pallas_call(children_kernel, name='children', out_shape=jax.ShapeDtype...  3.15 us
    unnamed x4, local copies, waits for them, and re-layouts  1.98 us

profile of v2, /device:TPU:1, one launch (start us, length us, event | category | flops | bytes accessed | tf_op | source)
XLA Modules:
  0.0 48.0 jit_solution(8299329147171608038)
XLA Ops:
  0.0 42.9 %main.1.local_ref = bf16[216,128]{1,0:T(8,128)(2,1)} custom-call(bf16[216,1024]{1,0:T(8,128)(2,1)} %child_hbm.1, bf16[216,128]{1,0:T(8,128)(2,1)} %incoming_hbm.1, bf16[8,216,216]{2,1,0:T(8,128)(2,1)} %m2m_hbm.1, bf16[10,216,216]{2,1,0:T(8,128)(2,1)} %ops_hbm.1, s32[160,128]{1,0:T(8,128)} %partners_hbm.1), custom_call_target="tpu_custom_call" | custom-call | tf_op jit(solution)/shard_map/main/pallas_call | solution.py:223
  42.9 0.0 copy-start
  42.9 1.2 %copy-done = bf16[8,216,216]{2,1,0:T(8,128)(2,1)S(1)} copy-done((bf16[8,216,216]{2,1,0:T(8,128)(2,1)S(1)}, bf16[8,216,216]{2,1,0:T(8,128)(2,1)}, u32[]{:S(2)}) %copy-start) | copy-done | bytes 746520
  44.0 0.0 copy-start.1
  44.0 0.8 %copy-done.1 = bf16[216,128]{1,0:T(8,128)(2,1)S(1)} copy-done((bf16[216,128]{1,0:T(8,128)(2,1)S(1)}, bf16[216,128]{1,0:T(8,128)(2,1)}, u32[]{:S(2)}) %copy-start.1) | copy-done | bytes 55320
  44.8 3.1 %children.1 = f32[216,1024]{1,0:T(8,128)} custom-call(bf16[216,128]{1,0:T(8,128)(2,1)S(1)} %copy-done.1, bf16[8,216,216]{2,1,0:T(8,128)(2,1)S(1)} %copy-done), custom_call_target="tpu_custom_call" | custom-call | tf_op jit(solution)/shard_map/children/pallas_call | solution.py:246
Async XLA Ops:
  42.9 1.2 %copy-start = (bf16[8,216,216]{2,1,0:T(8,128)(2,1)S(1)}, bf16[8,216,216]{2,1,0:T(8,128)(2,1)}, u32[]{:S(2)}) copy-start(bf16[8,216,216]{2,1,0:T(8,128)(2,1)} %l2l_ref.1) | copy-start | bytes 2239492
  44.0 0.8 %copy-start.1 = (bf16[216,128]{1,0:T(8,128)(2,1)S(1)}, bf16[216,128]{1,0:T(8,128)(2,1)}, u32[]{:S(2)}) copy-start(bf16[216,128]{1,0:T(8,128)(2,1)} %main.1.local_ref) | copy-start | bytes 165892

commit v3 on v2

v3 whole, which is shorter than its diff:
```python
import functools

import jax
import jax.numpy as jnp
from jax import lax
from jax.experimental import pallas as pl
from jax.experimental.pallas import tpu as pltpu
from jax.sharding import PartitionSpec as P

MESH = pl.DeviceIdType.MESH
F32 = jnp.float32
BF16 = jnp.bfloat16
VM = pl.BlockSpec(memory_space=pltpu.VMEM)
HB = pl.BlockSpec(memory_space=pltpu.HBM)
NONE = 64
LIMIT = 66_200_000


ORDER = [0, 4, 12, 1, 3, 8, 2, 5, 7, 13, 15, 9, 11, 6, 14, 10]
GROUPS = [(0, 1), (1, 3), (3, 5), (5, 7), (7, 9), (9, 11), (11, 13), (13, 15), (15, 16)]
AXES = ORDER[1:7]
SPLIT = 112


def moved(sub, i, sign):
    x, y = sub // 4, sub % 4
    return (x + sign * (i // 4) + 4) % 4 * 4 + (y + sign * (i % 4) + 4) % 4


def main_kernel(n_slab, n_sub, per, child_hbm, incoming_hbm, m2m_hbm, ops_hbm, l2l_hbm, partners_hbm, out_hbm,
                child_ref, incoming_ref, m2m_ref, ops_ref, l2l_ref, partners_ref, in_sem,
                block, win_ref, mine, words_ref, table_ref, table_smem, part_ref, got,
                w_send, w_recv, b_send, b_recv, h_send, h_recv, lo_send, lo_recv, hi_send, hi_recv, p_send, p_recv, own_sem, result_ref, out_sem):
    slab = lax.axis_index("slab")
    sub = lax.axis_index("sub")
    lower = (slab + n_slab - 1) % n_slab
    upper = (slab + 1) % n_slab
    rows, cells = block.shape

    loads = [
        pltpu.make_async_copy(source, target, in_sem.at[i])
        for i, (source, target) in enumerate(
            [(child_hbm, child_ref), (m2m_hbm, m2m_ref), (partners_hbm, partners_ref), (ops_hbm, ops_ref), (incoming_hbm, incoming_ref), (l2l_hbm, l2l_ref)]
        )
    ]
    for load in loads:
        load.start()
    barrier = pltpu.get_barrier_semaphore()
    for i in range(1, n_sub):
        pl.semaphore_signal(barrier, inc=1, device_id={"slab": slab, "sub": moved(sub, i, 1)}, device_id_type=MESH)
    for other in (lower, upper):
        pl.semaphore_signal(barrier, inc=1, device_id={"slab": other, "sub": sub}, device_id_type=MESH)

    source = lax.broadcasted_iota(jnp.int32, (256, 256), 0)
    lane = lax.broadcasted_iota(jnp.int32, (256, 256), 1)
    picks = []
    for h in range(4):
        o = jnp.bitwise_and(jnp.right_shift(lane, 5) - h, 3) + jnp.bitwise_and(jnp.right_shift(lane, 5), 4)
        picks.append(jnp.where(source == 8 * jnp.bitwise_and(lane, 31) + o, 1.0, 0.0).astype(BF16))
    loads[0].wait()
    spread = [jnp.dot(child_ref[:, 256 * h : 256 * (h + 1)], picks[h], preferred_element_type=F32).astype(BF16) for h in range(4)]
    loads[1].wait()
    quarter = lax.broadcasted_iota(jnp.int32, (rows, cells), 1) // 32
    total = jnp.zeros((rows, cells), F32)
    for r in range(4):
        turned = jnp.zeros((rows, cells), F32)
        for o in (r, r + 4):
            half = [piece[:, cells * (o // 4) : cells * (o // 4 + 1)].astype(F32) for piece in spread]
            column = half[(0 - r) % 4]
            for q in range(1, 4):
                column = jnp.where(quarter == q, half[(q - r) % 4], column)
            turned += jnp.dot(m2m_ref[o], column.astype(BF16), preferred_element_type=F32)
        total += turned if r == 0 else pltpu.roll(turned, cells - 32 * r, 1)
    moments = total.astype(BF16)
    block[...] = moments
    win_ref[n_sub] = moments
    pl.semaphore_wait(barrier, n_sub + 1)

    copies = []

    def send(src, dst, send_sem, recv_sem, device):
        copy = pltpu.make_async_remote_copy(
            src_ref=src, dst_ref=dst, send_sem=send_sem, recv_sem=recv_sem, device_id=device, device_id_type=MESH
        )
        copy.start()
        copies.append(copy)

    def expect(dst, send_sem, recv_sem, device):
        pltpu.make_async_remote_copy(
            src_ref=dst, dst_ref=dst, send_sem=send_sem, recv_sem=recv_sem, device_id=device, device_id_type=MESH
        ).wait_recv()

    def beside(first, last):
        for device, place, sends, recvs in ((lower, 2 * n_sub, lo_send, lo_recv), (upper, 0, hi_send, hi_recv)):
            send(
                win_ref.at[n_sub + first : n_sub + last],
                win_ref.at[place + first : place + last], sends.at[first], recvs.at[first], {"slab": device, "sub": sub},
            )

    beside(0, 1)
    for i in AXES:
        send(block, win_ref.at[n_sub + ORDER.index(i)], b_send.at[i], b_recv.at[i], {"slab": slab, "sub": moved(sub, i, 1)})
    halves = (pl.ds(0, SPLIT), pl.ds(SPLIT, rows - SPLIT))

    loads[2].wait()
    base = (slab - 1) * (n_sub * cells)
    lane = lax.broadcasted_iota(jnp.int32, (per, cells), 1)
    place = lax.broadcasted_iota(jnp.int32, (cells, cells), 0)
    across = lax.broadcasted_iota(jnp.int32, (cells, cells), 1)

    def words_for(group):
        codes, tables, which_of = [], [], []
        for j in range(8 * group, 8 * group + 8):
            p = partners_ref[per * j : per * (j + 1), :]
            rel = p - base
            brick = jnp.where(p >= 0, jnp.right_shift(rel, 7), NONE)
            which = jnp.zeros(p.shape, jnp.int32)
            packed = jnp.zeros(p.shape, jnp.int32)
            last = jnp.full((per, 1), -1, jnp.int32)
            for c in range(4):
                last = jnp.min(jnp.where(brick > last, brick, NONE), axis=1, keepdims=True)
                which = jnp.where((brick == last) & (brick < NONE), c, which)
                packed = jnp.where(lane % 4 == c, jnp.where(last < NONE, last, n_sub), packed)
            codes.append(jnp.where(p >= 0, jnp.bitwise_and(rel, 127) + 128, 0))
            tables.append(packed)
            which_of.append(which.astype(F32))
            which_of.append(jnp.zeros((16 - per, cells), F32))
        turned = jnp.transpose(jnp.concatenate(which_of, axis=0))
        back = jnp.zeros((cells, cells), F32)
        for j in range(8):
            left, right = [], []
            for k in range(per):
                left.append(jnp.where(jnp.bitwise_and(codes[j][k : k + 1, :], 127) == place, 1.0, 0.0).astype(BF16))
                right.append(jnp.where(across == 16 * j + k, turned, 0.0).astype(BF16))
            back += jnp.dot(jnp.concatenate(left, axis=1), jnp.concatenate(right, axis=0), preferred_element_type=F32)
        back = jnp.transpose(back).astype(jnp.int32)
        for j in range(8):
            mine[8 * group + j, 0:per, :] = codes[j] + jnp.bitwise_and(back[16 * j : 16 * j + per, :], 3) * 256 + tables[j] * 1024
            mine[8 * group + j, per:16, :] = jnp.zeros((16 - per, cells), jnp.int32)

    words_for(0)
    for first, last in GROUPS[1:]:
        for n in range(first, last):
            i = ORDER[n]
            origin = {"slab": slab, "sub": moved(sub, i, -1)}
            landed = win_ref.at[n_sub + n]
            if i in AXES:
                expect(landed, b_send.at[i], b_recv.at[i], origin)
                half, onward = (0, (1, 3, 2)) if i % 4 == 0 else (1, (4, 12, 8))
                for step in onward:
                    m = ORDER.index(i + step)
                    send(
                        landed.at[halves[half]], win_ref.at[n_sub + m, halves[half]], h_send.at[half, i + step], h_recv.at[half, i + step],
                        {"slab": slab, "sub": moved(sub, step, 1)},
                    )
            else:
                for half in range(2):
                    expect(landed.at[halves[half]], h_send.at[half, i], h_recv.at[half, i], origin)
        beside(first, last)
        if last == 7:
            words_for(1)
            for i in reversed(ORDER[1:]):
                to = moved(sub, i, 1)
                send(mine.at[to], words_ref.at[sub], w_send.at[i], w_recv.at[i], {"slab": slab, "sub": to})
            words_ref[sub] = mine[sub]
    for i in ORDER[1:]:
        origin = moved(sub, i, -1)
        expect(words_ref.at[origin], w_send.at[i], w_recv.at[i], {"slab": slab, "sub": origin})
    flat = jnp.concatenate([words_ref[j] for j in range(n_sub)], axis=0)
    brick = jnp.bitwise_and(jnp.right_shift(jnp.transpose(flat)[0:8, :], 10), 63)
    offset = jnp.bitwise_and(sub // 4 - jnp.right_shift(brick, 2), 3) * 4 + jnp.bitwise_and(sub - brick, 3)
    slot = jnp.zeros(brick.shape, jnp.int32)
    for n, i in enumerate(ORDER):
        slot = jnp.where(offset == i, n, slot)
    table_ref[...] = jnp.minimum(jnp.bitwise_and(brick, 48), 2 * n_sub) + slot
    to_smem = pltpu.make_async_copy(table_ref, table_smem, own_sem.at[0])
    to_smem.start()
    loads[3].wait()
    to_smem.wait()
    for first, last in GROUPS:
        expect(win_ref.at[2 * n_sub + first : 2 * n_sub + last], lo_send.at[first], lo_recv.at[first], {"slab": upper, "sub": sub})
        expect(win_ref.at[first:last], hi_send.at[first], hi_recv.at[first], {"slab": lower, "sub": sub})

    def columns_of(b, k):
        word = words_ref[b][k : k + 1, :]
        local = jnp.broadcast_to(jnp.bitwise_and(word, 127), (rows, cells))
        which = jnp.broadcast_to(jnp.bitwise_and(jnp.right_shift(word, 8), 3), (rows, cells)).astype(jnp.int16)
        there = jnp.broadcast_to(jnp.bitwise_and(word, 128), (rows, cells)).astype(jnp.int16)
        merged = win_ref[table_smem[0, b * 16 + k]]
        for c in range(1, 4):
            merged = jnp.where(which == c, win_ref[table_smem[c, b * 16 + k]], merged)
        got = jnp.take_along_axis(merged.astype(F32), local, axis=1, mode="promise_in_bounds").astype(BF16)
        return jnp.where(there != 0, got, jnp.zeros((), BF16))

    def part_copy(i, target):
        return pltpu.make_async_remote_copy(
            src_ref=part_ref.at[i], dst_ref=got.at[i], send_sem=p_send.at[i], recv_sem=p_recv.at[i],
            device_id={"slab": slab, "sub": target}, device_id_type=MESH,
        )

    def two_bricks(n, carry):
        ids = [15 - 2 * n, 14 - 2 * n]
        bricks = [moved(sub, i, 1) for i in ids]
        total = jnp.zeros((rows, 2 * cells), F32)
        for k in range(per):
            both = jnp.concatenate([columns_of(b, k) for b in bricks], axis=1)
            total += jnp.dot(ops_ref[k], both, preferred_element_type=F32)
        for q, (i, b) in enumerate(zip(ids, bricks)):
            part_ref[i] = total[:, q * cells : (q + 1) * cells].astype(BF16)

            @pl.when(i != 0)
            def _():
                part_copy(i, b).start()

        return carry

    lax.fori_loop(0, n_sub // 2, two_bricks, 0)
    loads[4].wait()
    total = part_ref[0].astype(F32)
    for i in reversed(ORDER[1:]):
        part_copy(i, moved(sub, i, -1)).wait_recv()
        total += got[i].astype(F32)
    locals_all = (incoming_ref[...].astype(F32) + total).astype(BF16)
    loads[5].wait()
    wide = 2 * cells
    stores = []
    for g in range(8 * cells // wide):
        row = lax.broadcasted_iota(jnp.int32, (cells, wide), 0)
        column = lax.broadcasted_iota(jnp.int32, (cells, wide), 1) + g * wide
        spread = jnp.where(jnp.right_shift(column, 3) == row, 1.0, 0.0).astype(BF16)
        repeated = jnp.dot(locals_all, spread, preferred_element_type=F32)
        octant = jnp.bitwise_and(lax.broadcasted_iota(jnp.int32, repeated.shape, 1), 7)
        result = jnp.zeros(repeated.shape, F32)
        for o in range(8):
            kept = jnp.where(octant == o, repeated, 0.0).astype(BF16)
            result += jnp.dot(l2l_ref[o], kept, preferred_element_type=F32)
        result_ref[:, g * wide : (g + 1) * wide] = result
        columns = pl.ds(g * wide, wide)
        stores.append(pltpu.make_async_copy(result_ref.at[:, columns], out_hbm.at[:, columns], out_sem.at[g]))
        stores[-1].start()
    for store in stores:
        store.wait()
    for i in ORDER[1:]:
        part_copy(i, moved(sub, i, 1)).wait_send()
    for copy in copies:
        copy.wait_send()


def solution(mesh):
    n_slab, n_sub = mesh.shape["slab"], mesh.shape["sub"]
    dma = pltpu.SemaphoreType.DMA

    def local(child_moments, incoming, m2m_ops, m2l_ops, l2l_ops, partners):
        rows = child_moments.shape[0]
        cells = incoming.shape[1]
        per = m2l_ops.shape[0]
        args = (child_moments, incoming, m2m_ops, m2l_ops, l2l_ops, partners)
        return pl.pallas_call(
            functools.partial(main_kernel, n_slab, n_sub, per),
            name="main",
            out_shape=jax.ShapeDtypeStruct((rows, 8 * cells), F32),
            in_specs=[HB] * 6,
            out_specs=HB,
            scratch_shapes=[pltpu.VMEM(a.shape, a.dtype) for a in args]
            + [
                dma((6,)),
                pltpu.VMEM((rows, cells), BF16),
                pltpu.VMEM((3 * n_sub, rows, cells), BF16),
                pltpu.VMEM((n_sub, 16, cells), jnp.int32),
                pltpu.VMEM((n_sub, 16, cells), jnp.int32),
                pltpu.VMEM((8, n_sub * 16), jnp.int32),
                pltpu.SMEM((8, n_sub * 16), jnp.int32),
                pltpu.VMEM((n_sub, rows, cells), BF16),
                pltpu.VMEM((n_sub, rows, cells), BF16),
            ]
            + [dma((16,))] * 4
            + [dma((2, 16))] * 2
            + [dma((16,))] * 6
            + [dma((1,)), pltpu.VMEM((rows, 8 * cells), F32), dma((4,))],
            compiler_params=pltpu.CompilerParams(collective_id=0, has_side_effects=True, vmem_limit_bytes=LIMIT),
        )(*args)

    in_specs = (
        P(None, ("slab", "sub")),
        P(None, ("slab", "sub")),
        P(),
        P("sub", None, None),
        P(),
        P(None, ("slab", "sub")),
    )
    return jax.shard_map(local, mesh=mesh, in_specs=in_specs, out_specs=P(None, ("slab", "sub")), check_vma=False)
```

time: 48.7 us -> 45.9 us (0.943)
  the two profiles are of different devices: /device:TPU:1 before, /device:TPU:2 now
where the time goes in v3:
time: 45.9 us; the launch traced here: 45.8 us
  Pallas kernels  43.6 us (95%)
  local copies, waits for them, and re-layouts  2.17 us (5%)
    pallas_call x1, Pallas kernels, local(): pl.pallas_call(functools.partial(main_kernel, n_slab, n_sub, per), name='...  43.6 us
    unnamed x1, local copies, waits for them, and re-layouts  2.17 us

profile of v3, /device:TPU:2, one launch (start us, length us, event | category | flops | bytes accessed | tf_op | source)
XLA Modules:
  0.0 45.8 jit_solution(13703048772917478882)
XLA Ops:
  0.0 43.6 %main.1 = f32[216,1024]{1,0:T(8,128)} custom-call(bf16[216,1024]{1,0:T(8,128)(2,1)} %child_hbm.1, bf16[216,128]{1,0:T(8,128)(2,1)} %incoming_hbm.1, bf16[8,216,216]{2,1,0:T(8,128)(2,1)} %m2m_hbm.1, bf16[10,216,216]{2,1,0:T(8,128)(2,1)} %ops_hbm.1, bf16[8,216,216]{2,1,0:T(8,128)(2,1)} %l2l_hbm.1, s32[160,128]{1,0:T(8,128)} %partners_hbm.1), custom_call_target="tpu_custom_call" | custom-call | tf_op jit(solution)/shard_map/main/pallas_call | solution.py:258
  43.6 2.2 %copy.8 = f32[216,1024]{1,0:T(8,128)} copy(f32[216,1024]{1,0:T(8,128)} %main.1) | data formatting | bytes 1769472

commit v4 on v3

--- a/solution.py
+++ b/solution.py
@@ -48,8 +48,18 @@
     barrier = pltpu.get_barrier_semaphore()
     for i in range(1, n_sub):
         pl.semaphore_signal(barrier, inc=1, device_id={"slab": slab, "sub": moved(sub, i, 1)}, device_id_type=MESH)
-    for other in (lower, upper):
-        pl.semaphore_signal(barrier, inc=1, device_id={"slab": other, "sub": sub}, device_id_type=MESH)
+    has_lower, has_upper = slab > 0, slab < n_slab - 1
+    for has, other in ((has_lower, lower), (has_upper, upper)):
+
+        @pl.when(has)
+        def _():
+            pl.semaphore_signal(barrier, inc=1, device_id={"slab": other, "sub": sub}, device_id_type=MESH)
+
+    for has, edge in ((has_lower, 0), (has_upper, 2 * n_sub)):
+
+        @pl.when(jnp.logical_not(has))
+        def _():
+            win_ref[edge : edge + n_sub] = jnp.zeros((n_sub, rows, cells), BF16)
 
     source = lax.broadcasted_iota(jnp.int32, (256, 256), 0)
     lane = lax.broadcasted_iota(jnp.int32, (256, 256), 1)
@@ -74,7 +84,7 @@
     moments = total.astype(BF16)
     block[...] = moments
     win_ref[n_sub] = moments
-    pl.semaphore_wait(barrier, n_sub + 1)
+    pl.semaphore_wait(barrier, n_sub - 1 + jnp.minimum(slab, 1) + jnp.minimum(n_slab - 1 - slab, 1))
 
     copies = []
 
@@ -90,12 +100,23 @@
             src_ref=dst, dst_ref=dst, send_sem=send_sem, recv_sem=recv_sem, device_id=device, device_id_type=MESH
         ).wait_recv()
 
+    def beside_copies(first, last):
+        return [
+            (
+                has,
+                pltpu.make_async_remote_copy(
+                    src_ref=win_ref.at[n_sub + first : n_sub + last], dst_ref=win_ref.at[place + first : place + last],
+                    send_sem=sends.at[first], recv_sem=recvs.at[first], device_id={"slab": device, "sub": sub}, device_id_type=MESH,
+                ),
+            )
+            for has, device, place, sends, recvs in (
+                (has_lower, lower, 2 * n_sub, lo_send, lo_recv), (has_upper, upper, 0, hi_send, hi_recv)
+            )
+        ]
+
     def beside(first, last):
-        for device, place, sends, recvs in ((lower, 2 * n_sub, lo_send, lo_recv), (upper, 0, hi_send, hi_recv)):
-            send(
-                win_ref.at[n_sub + first : n_sub + last],
-                win_ref.at[place + first : place + last], sends.at[first], recvs.at[first], {"slab": device, "sub": sub},
-            )
+        for has, copy in beside_copies(first, last):
+            pl.when(has)(copy.start)
 
     beside(0, 1)
     for i in AXES:
@@ -177,9 +198,15 @@
     to_smem.start()
     loads[3].wait()
     to_smem.wait()
-    for first, last in GROUPS:
-        expect(win_ref.at[2 * n_sub + first : 2 * n_sub + last], lo_send.at[first], lo_recv.at[first], {"slab": upper, "sub": sub})
-        expect(win_ref.at[first:last], hi_send.at[first], hi_recv.at[first], {"slab": lower, "sub": sub})
+    @pl.when(has_upper)
+    def _():
+        for first, last in GROUPS:
+            expect(win_ref.at[2 * n_sub + first : 2 * n_sub + last], lo_send.at[first], lo_recv.at[first], {"slab": upper, "sub": sub})
+
+    @pl.when(has_lower)
+    def _():
+        for first, last in GROUPS:
+            expect(win_ref.at[first:last], hi_send.at[first], hi_recv.at[first], {"slab": lower, "sub": sub})
 
     def columns_of(b, k):
         word = words_ref[b][k : k + 1, :]
@@ -242,6 +269,9 @@
         store.wait()
     for i in ORDER[1:]:
         part_copy(i, moved(sub, i, 1)).wait_send()
+    for first, last in GROUPS:
+        for has, copy in beside_copies(first, last):
+            pl.when(has)(copy.wait_send)
     for copy in copies:
         copy.wait_send()
 

time: 45.9 us -> 44.9 us (0.978)
  the two profiles are of different devices: /device:TPU:2 before, /device:TPU:1 now
where the time goes in v4:
time: 44.9 us; the launch traced here: 44.7 us
  Pallas kernels  42.5 us (95%)
  local copies, waits for them, and re-layouts  2.17 us (5%)
    pallas_call x1, Pallas kernels, local(): pl.pallas_call(functools.partial(main_kernel, n_slab, n_sub, per), name='...  42.5 us
    unnamed x1, local copies, waits for them, and re-layouts  2.17 us

profile of v4, /device:TPU:1, one launch (start us, length us, event | category | flops | bytes accessed | tf_op | source)
XLA Modules:
  0.0 44.7 jit_solution(12293175361591219999)
XLA Ops:
  0.0 42.5 %main.1 = f32[216,1024]{1,0:T(8,128)} custom-call(bf16[216,1024]{1,0:T(8,128)(2,1)} %child_hbm.1, bf16[216,128]{1,0:T(8,128)(2,1)} %incoming_hbm.1, bf16[8,216,216]{2,1,0:T(8,128)(2,1)} %m2m_hbm.1, bf16[10,216,216]{2,1,0:T(8,128)(2,1)} %ops_hbm.1, bf16[8,216,216]{2,1,0:T(8,128)(2,1)} %l2l_hbm.1, s32[160,128]{1,0:T(8,128)} %partners_hbm.1), custom_call_target="tpu_custom_call" | custom-call | tf_op jit(solution)/shard_map/main/pallas_call | solution.py:288
  42.5 2.2 %copy.8 = f32[216,1024]{1,0:T(8,128)} copy(f32[216,1024]{1,0:T(8,128)} %main.1) | data formatting | bytes 1769472

commit v5 on v4

--- a/solution.py
+++ b/solution.py
@@ -226,7 +226,7 @@
         )
 
     def two_bricks(n, carry):
-        ids = [15 - 2 * n, 14 - 2 * n]
+        ids = [jnp.bitwise_and(jnp.right_shift(jnp.int32(digits), 4 * n), 15) for digits in (0x4185D96A, 0x0C327FBE)]
         bricks = [moved(sub, i, 1) for i in ids]
         total = jnp.zeros((rows, 2 * cells), F32)
         for k in range(per):
@@ -249,18 +249,25 @@
         total += got[i].astype(F32)
     locals_all = (incoming_ref[...].astype(F32) + total).astype(BF16)
     loads[5].wait()
+    rolled = [pltpu.roll(locals_all.astype(F32), 32 * r, 1).astype(BF16) if r else locals_all for r in range(4)]
+    octants = [jnp.dot(l2l_ref[o], rolled[o % 4], preferred_element_type=F32) for o in range(8)]
     wide = 2 * cells
     stores = []
+    lane = lax.broadcasted_iota(jnp.int32, (wide, wide), 0)
+    column = lax.broadcasted_iota(jnp.int32, (wide, wide), 1)
     for g in range(8 * cells // wide):
-        row = lax.broadcasted_iota(jnp.int32, (cells, wide), 0)
-        column = lax.broadcasted_iota(jnp.int32, (cells, wide), 1) + g * wide
-        spread = jnp.where(jnp.right_shift(column, 3) == row, 1.0, 0.0).astype(BF16)
-        repeated = jnp.dot(locals_all, spread, preferred_element_type=F32)
-        octant = jnp.bitwise_and(lax.broadcasted_iota(jnp.int32, repeated.shape, 1), 7)
-        result = jnp.zeros(repeated.shape, F32)
-        for o in range(8):
-            kept = jnp.where(octant == o, repeated, 0.0).astype(BF16)
-            result += jnp.dot(l2l_ref[o], kept, preferred_element_type=F32)
+        o = jnp.bitwise_and(jnp.right_shift(lane, 5) - g, 3) + jnp.bitwise_and(jnp.right_shift(lane, 5), 4)
+        spread = jnp.where(column == 8 * jnp.bitwise_and(lane, 31) + o, 1.0, 0.0).astype(BF16)
+        both = []
+        for half in range(2):
+            mixed = octants[(0 - g) % 4 + 4 * half]
+            for q in range(1, 4):
+                mixed = jnp.where(quarter == q, octants[(q - g) % 4 + 4 * half], mixed)
+            both.append(mixed)
+        mixed = jnp.concatenate(both, axis=1)
+        high = mixed.astype(BF16)
+        low = (mixed - high.astype(F32)).astype(BF16)
+        result = jnp.dot(high, spread, preferred_element_type=F32) + jnp.dot(low, spread, preferred_element_type=F32)
         result_ref[:, g * wide : (g + 1) * wide] = result
         columns = pl.ds(g * wide, wide)
         stores.append(pltpu.make_async_copy(result_ref.at[:, columns], out_hbm.at[:, columns], out_sem.at[g]))

time: 44.9 us -> 43.1 us (0.960)
  Pallas kernels: 42.5 us -> 40.8 us
    pallas_call x1, Pallas kernels: 42.5 us -> 40.8 us  [local(): pl.pallas_call(functools.partial(main_kernel, n_slab, n_sub, per), name='...]
where the time goes in v5:
time: 43.1 us; the launch traced here: 42.9 us
  Pallas kernels  40.8 us (95%)
  local copies, waits for them, and re-layouts  2.17 us (5%)
    pallas_call x1, Pallas kernels, local(): pl.pallas_call(functools.partial(main_kernel, n_slab, n_sub, per), name='...  40.8 us
    unnamed x1, local copies, waits for them, and re-layouts  2.17 us

profile of v5, /device:TPU:1, one launch (start us, length us, event | category | flops | bytes accessed | tf_op | source)
XLA Modules:
  0.0 42.9 jit_solution(11919008813614914385)
XLA Ops:
  0.0 40.8 %main.1 = f32[216,1024]{1,0:T(8,128)} custom-call(bf16[216,1024]{1,0:T(8,128)(2,1)} %child_hbm.1, bf16[216,128]{1,0:T(8,128)(2,1)} %incoming_hbm.1, bf16[8,216,216]{2,1,0:T(8,128)(2,1)} %m2m_hbm.1, bf16[10,216,216]{2,1,0:T(8,128)(2,1)} %ops_hbm.1, bf16[8,216,216]{2,1,0:T(8,128)(2,1)} %l2l_hbm.1, s32[160,128]{1,0:T(8,128)} %partners_hbm.1), custom_call_target="tpu_custom_call" | custom-call | tf_op jit(solution)/shard_map/main/pallas_call | solution.py:295
  40.8 2.2 %copy.8 = f32[216,1024]{1,0:T(8,128)} copy(f32[216,1024]{1,0:T(8,128)} %main.1) | data formatting | bytes 1769472

commit v6 on v5

--- a/solution.py
+++ b/solution.py
@@ -17,7 +17,7 @@
 
 
 ORDER = [0, 4, 12, 1, 3, 8, 2, 5, 7, 13, 15, 9, 11, 6, 14, 10]
-GROUPS = [(0, 1), (1, 3), (3, 5), (5, 7), (7, 9), (9, 11), (11, 13), (13, 15), (15, 16)]
+GROUPS = [(0, 1), (1, 5), (5, 7), (7, 11), (11, 15), (15, 16)]
 AXES = ORDER[1:7]
 SPLIT = 112
 

time: 43.1 us -> 43 us (level)
  no operation moved by 1% of the time
where the time goes in v6:
time: 43 us; the launch traced here: 42.9 us
  Pallas kernels  40.7 us (95%)
  local copies, waits for them, and re-layouts  2.17 us (5%)
    pallas_call x1, Pallas kernels, local(): pl.pallas_call(functools.partial(main_kernel, n_slab, n_sub, per), name='...  40.7 us
    unnamed x1, local copies, waits for them, and re-layouts  2.17 us

profile of v6, /device:TPU:1, one launch (start us, length us, event | category | flops | bytes accessed | tf_op | source)
XLA Modules:
  0.0 42.9 jit_solution(3596736123733783877)
XLA Ops:
  0.0 40.7 %main.1 = f32[216,1024]{1,0:T(8,128)} custom-call(bf16[216,1024]{1,0:T(8,128)(2,1)} %child_hbm.1, bf16[216,128]{1,0:T(8,128)(2,1)} %incoming_hbm.1, bf16[8,216,216]{2,1,0:T(8,128)(2,1)} %m2m_hbm.1, bf16[10,216,216]{2,1,0:T(8,128)(2,1)} %ops_hbm.1, bf16[8,216,216]{2,1,0:T(8,128)(2,1)} %l2l_hbm.1, s32[160,128]{1,0:T(8,128)} %partners_hbm.1), custom_call_target="tpu_custom_call" | custom-call | tf_op jit(solution)/shard_map/main/pallas_call | solution.py:295
  40.7 2.2 %copy.8 = f32[216,1024]{1,0:T(8,128)} copy(f32[216,1024]{1,0:T(8,128)} %main.1) | data formatting | bytes 1769472
